TPU v7x, 256 devices: a whole 4x4x8 slice. The times are simulated.
256 devices in a mesh: tm: 64 (over z, x, core), blk: 4 (over y).
Axes of the slice: x: 4, y: 4, z: 8, core: 2. Of those that a mesh axis runs over, the one named last changes fastest.
Arguments:
- prior_mean: float32 [512], replicated, may hold values from -6 to 6
- after_mean: float32 [512], replicated, may hold values from -6 to 6
- filter_map: float32 [128, 512, 512], P('tm', 'blk'), may hold values from -1 to 1.5
- smoother_gain: float32 [128, 512, 512], P('tm', 'blk'), may hold values from -1 to 1.5
- smoother_map: float32 [128, 512, 512], P('tm', 'blk'), may hold values from -1 to 1.5
- obs_gain: float32 [128, 512, 128], P('tm', 'blk'), may hold values from -0.5 to 0.5
- observations: float32 [128, 128], P('tm'), may hold values from -6 to 6
Outputs:
- filtered: float32 [128, 512], P('tm', 'blk')
- smoothed: float32 [128, 512], P('tm', 'blk')
All inputs are finite; a program needn't handle non-finite values.
Results may differ from a plain program's by a relative error of at most 0.0003.
Values sent between devices are 32-bit elements; how exact they have to be, the bound alone decides.
A program may use at most 128 MiB of HBM per device.

v0:
```python
import jax
import jax.numpy as jnp
from jax import lax
from jax.sharding import Mesh
from jax.sharding import PartitionSpec as P

TM = ("tm_0", "tm_1", "tm_2")


def neutral_like(value, identity):
    return jax.tree.map(
        lambda part, zero: jnp.zeros_like(part) + jnp.asarray(zero, part.dtype), value, identity
    )


def prefix_by_axis(value, axes, combine, identity, reverse):
    before = start = neutral_like(value, identity)
    so_far = value
    for axis in reversed(axes):
        length, index = (lax.axis_size(axis), lax.axis_index(axis))
        pieces = jax.tree.map(lambda part: lax.all_gather(part, axis), so_far)
        inside, so_far = (start, start)
        for k in reversed(range(length)) if reverse else range(length):
            passed = k > index if reverse else k < index
            so_far = combine(so_far, jax.tree.map(lambda part: part[k], pieces))
            inside = jax.tree.map(lambda new, old: jnp.where(passed, new, old), so_far, inside)
        before = combine(inside, before)
    return before


def chain_combine(earlier, later):
    highest = lax.Precision.HIGHEST
    joined_map = jnp.dot(later[0], earlier[0], precision=highest)
    joined_offset = jnp.dot(later[0], earlier[1], precision=highest) + later[1]
    return (joined_map, joined_offset)


def shards(prior_mean, after_mean, filter_map, smoother_gain, smoother_map, obs_gain, observations):
    highest = lax.Precision.HIGHEST
    steps = filter_map.shape[0]
    rows = filter_map.shape[1]
    width = filter_map.shape[2]
    first_row = lax.axis_index("blk") * rows
    drive_rows = jnp.einsum("tro,to->tr", obs_gain, observations, precision=highest)
    full_filter, full_gain, drive = (
        lax.all_gather(filter_map, "blk", axis=1, tiled=True),
        lax.all_gather(smoother_gain, "blk", axis=1, tiled=True),
        lax.all_gather(drive_rows, "blk", axis=1, tiled=True),
    )
    identity = jnp.eye(width, dtype=jnp.float32)
    nothing = jnp.zeros((width,), jnp.float32)
    offset = nothing
    for index in range(steps):
        offset = jnp.dot(full_filter[index], offset, precision=highest) + drive[index]
    composite = full_filter[steps - 1]
    index = 0
    composite = jnp.dot(composite, full_filter[index], precision=highest)
    total = prefix_by_axis((composite, offset), TM, chain_combine, (identity, nothing), False)
    entering = jnp.dot(total[0], prior_mean, precision=highest) + total[1]
    current = entering
    filtered_list = []
    for index in range(steps):
        current = jnp.dot(full_filter[index], current, precision=highest) + drive[index]
        filtered_list.append(current)
    filtered_full = jnp.stack(filtered_list, axis=0)
    filtered_rows = lax.dynamic_slice_in_dim(filtered_full, first_row, rows, 1)
    pulled_rows = jnp.einsum("trk,tk->tr", smoother_map, filtered_full, precision=highest)
    pulled = lax.all_gather(pulled_rows, "blk", axis=1, tiled=True)
    offset = nothing
    for index in range(steps - 1, -1, -1):
        offset = jnp.dot(full_gain[index], offset, precision=highest) + pulled[index]
    composite = full_gain[0]
    index = 1
    composite = jnp.dot(composite, full_gain[index], precision=highest)
    total = prefix_by_axis((composite, offset), TM, chain_combine, (identity, nothing), True)
    leaving = jnp.dot(total[0], after_mean, precision=highest) + total[1]
    current = leaving
    smoothed_list = []
    for index in range(steps - 1, -1, -1):
        current = jnp.dot(full_gain[index], current, precision=highest) + pulled[index]
        smoothed_list.append(current)
    smoothed_full = jnp.stack(smoothed_list[::-1], axis=0)
    smoothed_rows = lax.dynamic_slice_in_dim(smoothed_full, first_row, rows, 1)
    return (filtered_rows, smoothed_rows)


def solution(mesh):
    torus = Mesh(mesh.devices.reshape(8, 4, 2, mesh.shape["blk"]), ("tm_0", "tm_1", "tm_2", "blk"))
    in_specs = (
        P(),
        P(),
        P(TM, "blk", None),
        P(TM, "blk", None),
        P(TM, "blk", None),
        P(TM, "blk", None),
        P(TM, None),
    )
    out_specs = (P(TM, "blk"), P(TM, "blk"))
    return jax.shard_map(
        shards, mesh=torus, in_specs=in_specs, out_specs=out_specs, check_vma=False
    )
```

profile of v0, /device:TPU:1, one launch (start us, length us, event | category | flops | bytes accessed | tf_op | source)
XLA Modules:
  0.0 462.8 jit_solution(7283257458123513231)
XLA Ops:
  8.7 38.1 %all-gather.27.cloned.1.call-done = f32[2,512,512]{2,1,0:T(8,128)} async-done(((f32[2,128,512]{2,1,0:T(8,128)}), f32[2,512,512]{2,1,0:T(8,128)}) %all-gather.27.cloned.1.call-update) | async-done | bytes 2097168 | tf_op jit(solution)/shard_map/all_gather | solution.py:46
  46.8 4.4 fusion.142
  51.2 30.8 %all-gather.29.cloned.1.call-done = f32[2,512,512]{2,1,0:T(8,128)} async-done(((f32[2,128,512]{2,1,0:T(8,128)}), f32[2,512,512]{2,1,0:T(8,128)}) %all-gather.29.cloned.1.call-update) | async-done | bytes 2097168 | tf_op jit(solution)/shard_map/all_gather | solution.py:47
  82.0 4.4 fusion.147
  86.5 14.2 %all-gather.31.cloned.1.call-done = f32[1024,512]{1,0:T(8,128)} async-done(((f32[512,512]{1,0:T(8,128)}), f32[1024,512]{1,0:T(8,128)}) %all-gather.31.cloned.1.call-update) | async-done | bytes 2097168 | tf_op jit(solution)/shard_map/all_gather | solution.py:21
  102.9 4.4 fusion.136
  107.4 12.2 %all-gather.37.cloned.1.call-done = f32[1024,512]{1,0:T(8,128)} async-done(((f32[512,512]{1,0:T(8,128)}), f32[1024,512]{1,0:T(8,128)}) %all-gather.37.cloned.1.call-update) | async-done | bytes 2097168 | tf_op jit(solution)/shard_map/all_gather | solution.py:21
  121.8 4.4 fusion.84
  126.4 46.0 %all-gather.33.cloned.1.call-done = f32[2048,512]{1,0:T(8,128)} async-done(((f32[512,512]{1,0:T(8,128)}), f32[2048,512]{1,0:T(8,128)}) %all-gather.33.cloned.1.call-update) | async-done | bytes 4194320 | tf_op jit(solution)/shard_map/all_gather | solution.py:21
  175.8 3.1 fusion.121
  182.7 2.8 fusion.129
  186.0 8.1 %all_gather.91 = f32[2,512]{1,0:T(2,128)S(1)} all-gather(f32[2,128]{1,0:T(2,128)S(1)} %bitcast.347), channel_id=1, replica_groups=mesh['tm_0'=8,'tm_1'=4,'tm_2'=2,'blk'=4] {'blk'}, dimensions={1}, use_global_device_ids=true | all-gather | bytes 5120 | tf_op jit(solution)/shard_map/all_gather | solution.py:48
  198.5 4.2 all-gather.12
  203.6 21.6 %all-gather.39.cloned.1.call-done = f32[2048,512]{1,0:T(8,128)} async-done(((f32[512,512]{1,0:T(8,128)}), f32[2048,512]{1,0:T(8,128)}) %all-gather.39.cloned.1.call-update) | async-done | bytes 4194320 | tf_op jit(solution)/shard_map/all_gather | solution.py:21
  228.5 3.1 fusion.69
  235.5 2.8 fusion.77
  238.4 2.5 fusion.134
  243.2 9.4 %all-gather.13 = f32[4,1,512]{2,1,0:T(1,128)S(1)} all-gather(f32[1,1,512]{2,1,0:T(1,128)S(1)} %bitcast.331), channel_id=6, replica_groups=mesh['tm_0'=8,'tm_1'=4,'tm_2'=2,'blk'=4] {'tm_1'}, dimensions={0}, use_global_device_ids=true | all-gather | bytes 10240 | tf_op jit(solution)/shard_map/all_gather | solution.py:21
  261.7 22.3 %all-gather.14 = f32[8,1,512]{2,1,0:T(1,128)S(1)} all-gather(f32[1,1,512]{2,1,0:T(1,128)S(1)} %bitcast.342), channel_id=7, replica_groups=mesh['tm_0'=8,'tm_1'=4,'tm_2'=2,'blk'=4] {'tm_0'}, dimensions={0}, use_global_device_ids=true | all-gather | bytes 18432 | tf_op jit(solution)/shard_map/all_gather | solution.py:21
  284.0 2.4 fusion.67
  287.4 3.0 fusion.6
  290.4 3.0 fusion.20
  293.4 28.4 %all-gather.35.cloned.1.call-done = f32[4096,512]{1,0:T(8,128)} async-done(((f32[512,512]{1,0:T(8,128)}), f32[4096,512]{1,0:T(8,128)}) %all-gather.35.cloned.1.call-update) | async-done | bytes 8388624 | tf_op jit(solution)/shard_map/all_gather | solution.py:21
  324.1 2.3 fusion.93
  326.5 2.5 fusion.97
  361.3 8.5 %all_gather.105 = f32[2,512]{1,0:T(2,128)S(1)} all-gather(f32[2,128]{1,0:T(2,128)S(1)} %bitcast.346), channel_id=1, replica_groups=mesh['tm_0'=8,'tm_1'=4,'tm_2'=2,'blk'=4] {'blk'}, dimensions={1}, use_global_device_ids=true | all-gather | bytes 5120 | tf_op jit(solution)/shard_map/all_gather | solution.py:68
  370.8 3.6 all-gather.15
  375.4 9.5 %all-gather.16 = f32[4,1,512]{2,1,0:T(1,128)S(1)} all-gather(f32[1,1,512]{2,1,0:T(1,128)S(1)} %bitcast.330), channel_id=12, replica_groups=mesh['tm_0'=8,'tm_1'=4,'tm_2'=2,'blk'=4] {'tm_1'}, dimensions={0}, use_global_device_ids=true | all-gather | bytes 10240 | tf_op jit(solution)/shard_map/all_gather | solution.py:21
  387.9 19.5 %all-gather.17 = f32[8,1,512]{2,1,0:T(1,128)S(1)} all-gather(f32[1,1,512]{2,1,0:T(1,128)S(1)} %bitcast.339), channel_id=13, replica_groups=mesh['tm_0'=8,'tm_1'=4,'tm_2'=2,'blk'=4] {'tm_0'}, dimensions={0}, use_global_device_ids=true | all-gather | bytes 18432 | tf_op jit(solution)/shard_map/all_gather | solution.py:21
  408.7 7.8 %all-gather.41.cloned.1.call-done = f32[4096,512]{1,0:T(8,128)} async-done(((f32[512,512]{1,0:T(8,128)}), f32[4096,512]{1,0:T(8,128)}) %all-gather.41.cloned.1.call-update) | async-done | bytes 8388624 | tf_op jit(solution)/shard_map/all_gather | solution.py:21
  418.8 2.3 fusion.41
  421.2 2.5 fusion.45
  (206 shorter events, 113.7 us)
Async XLA Ops:
  7.2 353.7 %copy-start = (f32[2,128,512]{2,1,0:T(8,128)S(1)}, f32[2,128,512]{2,1,0:T(8,128)}, u32[]{:S(2)}) copy-start(f32[2,128,512]{2,1,0:T(8,128)} %param.11) | copy-start | bytes 1572868
  7.2 39.6 %all-gather.27.cloned.1.call-start = ((), (), s32[]{:S(2)}) async-start(), calls=%async_computation | async-start | bytes 2621440 | tf_op jit(solution)/shard_map/all_gather | solution.py:46
  7.9 74.1 %all-gather.29.cloned.1.call-start = ((), (), s32[]{:S(2)}) async-start(), calls=%async_computation.1 | async-start | bytes 2621440 | tf_op jit(solution)/shard_map/all_gather | solution.py:47
  8.7 92.0 %all-gather.31.cloned.1.call-start = ((), (), s32[]{:S(2)}) async-start(), calls=%async_computation.2 | async-start | bytes 3145728 | tf_op jit(solution)/shard_map/all_gather | solution.py:21
  51.2 68.4 %all-gather.37.cloned.1.call-start = ((), (), s32[]{:S(2)}) async-start(), calls=%async_computation.5 | async-start | bytes 3145728 | tf_op jit(solution)/shard_map/all_gather | solution.py:21
  86.4 86.0 %all-gather.33.cloned.1.call-start = ((), (), s32[]{:S(2)}) async-start(), calls=%async_computation.3 | async-start | bytes 5242880 | tf_op jit(solution)/shard_map/all_gather | solution.py:21
  102.9 23.3 %copy-start.13 = (f32[512,512]{1,0:T(8,128)}, f32[512,512]{1,0:T(8,128)S(1)}, u32[]{:S(2)}) copy-start(f32[512,512]{1,0:T(8,128)S(1)} %fusion.35) | copy-start | bytes 3145732
  107.3 117.9 %all-gather.39.cloned.1.call-start = ((), (), s32[]{:S(2)}) async-start(), calls=%async_computation.6 | async-start | bytes 5242880 | tf_op jit(solution)/shard_map/all_gather | solution.py:21
  121.8 53.0 %copy-start.16 = (f32[512,512]{1,0:T(8,128)}, f32[512,512]{1,0:T(8,128)S(1)}, u32[]{:S(2)}) copy-start(f32[512,512]{1,0:T(8,128)S(1)} %fusion.31) | copy-start | bytes 3145732
  126.2 195.6 %all-gather.35.cloned.1.call-start = ((), (), s32[]{:S(2)}) async-start(), calls=%async_computation.4 | async-start | bytes 9437184 | tf_op jit(solution)/shard_map/all_gather | solution.py:21
  172.4 7.4 %copy-start.7 = (f32[2048,512]{1,0:T(8,128)S(1)}, f32[2048,512]{1,0:T(8,128)}, u32[]{:S(2)}) copy-start(f32[2048,512]{1,0:T(8,128)} %all-gather.33.cloned.1.call-done) | copy-start | bytes 12582916
  179.8 22.9 %copy-start.3 = (f32[2,512,512]{2,1,0:T(8,128)S(1)}, f32[2,512,512]{2,1,0:T(8,128)}, u32[]{:S(2)}) copy-start(f32[2,512,512]{2,1,0:T(8,128)} %all-gather.29.cloned.1.call-done) | copy-start | bytes 6291460
  185.6 231.0 %all-gather.41.cloned.1.call-start = ((), (), s32[]{:S(2)}) async-start(), calls=%async_computation.7 | async-start | bytes 9437184 | tf_op jit(solution)/shard_map/all_gather | solution.py:21
  225.2 7.4 %copy-start.5 = (f32[2048,512]{1,0:T(8,128)S(1)}, f32[2048,512]{1,0:T(8,128)}, u32[]{:S(2)}) copy-start(f32[2048,512]{1,0:T(8,128)} %all-gather.39.cloned.1.call-done) | copy-start | bytes 12582916
  238.3 16.9 %copy-start.14 = (f32[512,512]{1,0:T(8,128)S(1)}, f32[512,512]{1,0:T(8,128)}, u32[]{:S(2)}) copy-start(f32[512,512]{1,0:T(8,128)} %copy-done.13) | copy-start | bytes 3145732
  238.3 16.9 %copy-start.15 = (f32[512,512]{1,0:T(8,128)S(1)}, f32[512,512]{1,0:T(8,128)}, u32[]{:S(2)}) copy-start(f32[512,512]{1,0:T(8,128)} %fusion.136) | copy-start | bytes 3145732
  238.3 18.1 %copy-start.17 = (f32[512,512]{1,0:T(8,128)S(1)}, f32[512,512]{1,0:T(8,128)}, u32[]{:S(2)}) copy-start(f32[512,512]{1,0:T(8,128)} %copy-done.16) | copy-start | bytes 3145732
  238.3 18.1 %copy-start.18 = (f32[512,512]{1,0:T(8,128)S(1)}, f32[512,512]{1,0:T(8,128)}, u32[]{:S(2)}) copy-start(f32[512,512]{1,0:T(8,128)} %fusion.84) | copy-start | bytes 3145732
  240.8 16.8 %copy-start.8 = (f32[2048,512]{1,0:T(8,128)S(1)}, f32[2048,512]{1,0:T(8,128)}, u32[]{:S(2)}) copy-start(f32[2048,512]{1,0:T(8,128)} %all-gather.33.cloned.1.call-done) | copy-start | bytes 12582916
  256.4 31.0 %copy-start.10 = (f32[512,512]{1,0:T(8,128)S(1)}, f32[512,512]{1,0:T(8,128)}, u32[]{:S(2)}) copy-start(f32[512,512]{1,0:T(8,128)} %copy-done.9) | copy-start | bytes 3145732
  256.4 31.0 %copy-start.12 = (f32[512,512]{1,0:T(8,128)S(1)}, f32[512,512]{1,0:T(8,128)}, u32[]{:S(2)}) copy-start(f32[512,512]{1,0:T(8,128)} %copy-done.11) | copy-start | bytes 3145732
  256.4 31.0 %copy-start.25 = (f32[512,512]{1,0:T(8,128)S(1)}, f32[512,512]{1,0:T(8,128)}, u32[]{:S(2)}) copy-start(f32[512,512]{1,0:T(8,128)} %fusion.129) | copy-start | bytes 3145732
  256.4 31.0 %copy-start.27 = (f32[512,512]{1,0:T(8,128)S(1)}, f32[512,512]{1,0:T(8,128)}, u32[]{:S(2)}) copy-start(f32[512,512]{1,0:T(8,128)} %copy-done.26) | copy-start | bytes 3145732
  257.6 32.8 %copy-start.31 = (f32[512,512]{1,0:T(8,128)}, f32[512,512]{1,0:T(8,128)S(1)}, u32[]{:S(2)}) copy-start(f32[512,512]{1,0:T(8,128)S(1)} %fusion.15) | copy-start | bytes 3145732
  284.0 6.4 %copy-start.22 = (f32[512,512]{1,0:T(8,128)S(1)}, f32[512,512]{1,0:T(8,128)}, u32[]{:S(2)}) copy-start(f32[512,512]{1,0:T(8,128)} %copy-done.21) | copy-start | bytes 3145732
  321.8 18.5 %copy-start.30 = (f32[512,512]{1,0:T(8,128)S(1)}, f32[512,512]{1,0:T(8,128)}, u32[]{:S(2)}) copy-start(f32[512,512]{1,0:T(8,128)} %fusion.6) | copy-start | bytes 3145732
  324.1 17.1 %copy-start.2 = (f32[4096,512]{1,0:T(8,128)S(1)}, f32[4096,512]{1,0:T(8,128)}, u32[]{:S(2)}) copy-start(f32[4096,512]{1,0:T(8,128)} %all-gather.35.cloned.1.call-done) | copy-start | bytes 25165828
  353.6 20.8 %copy-start.33 = (f32[1024,512]{1,0:T(8,128)S(1)}, f32[1024,512]{1,0:T(8,128)}, u32[]{:S(2)}) copy-start(f32[1024,512]{1,0:T(8,128)} %all-gather.37.cloned.1.call-done) | copy-start | bytes 6291460
  355.9 28.9 %copy-start.6 = (f32[2048,512]{1,0:T(8,128)S(1)}, f32[2048,512]{1,0:T(8,128)}, u32[]{:S(2)}) copy-start(f32[2048,512]{1,0:T(8,128)} %all-gather.39.cloned.1.call-done) | copy-start | bytes 12582916
  358.8 48.9 %copy-start.32 = (f32[512,512]{1,0:T(8,128)S(1)}, f32[512,512]{1,0:T(8,128)}, u32[]{:S(2)}) copy-start(f32[512,512]{1,0:T(8,128)} %copy-done.31) | copy-start | bytes 3145732
  416.5 18.3 %copy-start.24 = (f32[512,512]{1,0:T(8,128)S(1)}, f32[512,512]{1,0:T(8,128)}, u32[]{:S(2)}) copy-start(f32[512,512]{1,0:T(8,128)} %fusion.20) | copy-start | bytes 3145732
  418.8 17.0 %copy-start.1 = (f32[4096,512]{1,0:T(8,128)S(1)}, f32[4096,512]{1,0:T(8,128)}, u32[]{:S(2)}) copy-start(f32[4096,512]{1,0:T(8,128)} %all-gather.41.cloned.1.call-done) | copy-start | bytes 25165828
  (14 other events, 48.1 us)
Sparse Core Ops, SparseCore 0:
  9.8 36.9 all-gather.26
  48.6 33.3 all-gather.28
  83.8 16.8 all-gather.30
  102.3 17.1 all-gather.36
  121.2 51.1 all-gather.32
  174.1 51.0 all-gather.38
  227.0 94.7 all-gather.34
  323.6 92.9 all-gather.40
where the time goes:
time: 471 us; the launch traced here: 463 us
  waiting for transfers between devices  200 us (42%)
  matrix products  155 us (33%)
  blocking collectives  85.1 us (18%)
  between operations  15.1 us (3%)
  local copies, waits for them, and re-layouts  6.15 us (1%)
    all_gather x6, waiting for transfers between devices, prefix_by_axis(): pieces = jax.tree.map(lambda part: lax.all_gather(part, axis), so_far)  130 us
    dot_general x34, matrix products, chain_combine(): joined_map = jnp.dot(later[0], earlier[0], precision=highest)  74.4 us
    all_gather x6, blocking collectives, prefix_by_axis(): pieces = jax.tree.map(lambda part: lax.all_gather(part, axis), so_far)  68.5 us
    dot_general x34, matrix products, chain_combine(): joined_offset = jnp.dot(later[0], earlier[1], precision=highest) + later[1]  58.5 us
    all_gather x1, waiting for transfers between devices, shards(): lax.all_gather(filter_map, 'blk', axis=1, tiled=True)  38.1 us
    all_gather x1, waiting for transfers between devices, shards(): lax.all_gather(smoother_gain, 'blk', axis=1, tiled=True)  30.8 us
  transfers between devices with their start and end apart: 8, of which 8 were waited for; matrix products, arithmetic and copies ran while one was open for 25% of the time, Pallas kernels for 0%

commit v1 on v0

--- a/solution.py
+++ b/solution.py
@@ -5,6 +5,32 @@
 from jax.sharding import PartitionSpec as P
 
 TM = ("tm_0", "tm_1", "tm_2")
+
+
+def process_islands(xin, axis_name):
+    taken_in = jax.lax.psum(1, axis_name=axis_name)
+    local_out = jax.lax.axis_index(axis_name)
+    met_up, aux, long_array = (taken_in, local_out, xin.shape[1])
+    rack = [h * met_up if src_i == 1 else h for src_i, h in enumerate(xin.shape)]
+    clean = lax.dynamic_update_slice_in_dim(
+        jnp.zeros(rack, xin.dtype), xin, aux * long_array, axis=1
+    )
+    last = x_now = xin
+    for num in range(1, met_up // 2 + 1):
+        last = jax.lax.ppermute(
+            last, axis_name, [(src_i, (src_i + 1) % met_up) for src_i in range(met_up)]
+        )
+        clean = lax.dynamic_update_slice_in_dim(
+            clean, last, (aux - num) % met_up * long_array, axis=1
+        )
+        if 2 * num < met_up:
+            x_now = jax.lax.ppermute(
+                x_now, axis_name, perm=[(src_i, (src_i - 1) % met_up) for src_i in range(met_up)]
+            )
+            clean = lax.dynamic_update_slice_in_dim(
+                clean, x_now, (aux + num) % met_up * long_array, axis=1
+            )
+    return clean
 
 
 def neutral_like(value, identity):
@@ -44,7 +70,7 @@
     drive_rows = jnp.einsum("tro,to->tr", obs_gain, observations, precision=highest)
     full_filter, full_gain, drive = (
         lax.all_gather(filter_map, "blk", axis=1, tiled=True),
-        lax.all_gather(smoother_gain, "blk", axis=1, tiled=True),
+        process_islands(smoother_gain, "blk"),
         lax.all_gather(drive_rows, "blk", axis=1, tiled=True),
     )
     identity = jnp.eye(width, dtype=jnp.float32)

time: 471 us -> 514 us (1.091)
  the two profiles are of different devices: /device:TPU:1 before, /device:TPU:32 now
where the time goes in v1:
time: 514 us; the launch traced here: 506 us
  waiting for transfers between devices  229 us (45%)
  matrix products  152 us (30%)
  blocking collectives  92.1 us (18%)
  between operations  15.4 us (3%)
  local copies, waits for them, and re-layouts  11.7 us (2%)
    all_gather x6, waiting for transfers between devices, prefix_by_axis(): pieces = jax.tree.map(lambda part: lax.all_gather(part, axis), so_far)  192 us
    dot_general x34, matrix products, chain_combine(): joined_map = jnp.dot(later[0], earlier[0], precision=highest)  78.9 us
    all_gather x6, blocking collectives, prefix_by_axis(): pieces = jax.tree.map(lambda part: lax.all_gather(part, axis), so_far)  72.5 us
    dot_general x34, matrix products, chain_combine(): joined_offset = jnp.dot(later[0], earlier[1], precision=highest) + later[1]  55.5 us
    ppermute x2, waiting for transfers between devices, process_islands(): jax.lax.ppermute(last, axis_name, [(src_i, (src_i + 1) % met_up) for src_...  33.8 us
  transfers between devices with their start and end apart: 10, of which 9 were waited for; matrix products, arithmetic and copies ran while one was open for 18% of the time, Pallas kernels for 0%

profile of v1, /device:TPU:32, one launch (start us, length us, event | category | flops | bytes accessed | tf_op | source)
XLA Modules:
  0.0 505.6 jit_solution(1677800865238200108)
XLA Ops:
  11.3 11.9 %collective-permute-done = f32[2,128,512]{2,1,0:T(8,128)S(1)} collective-permute-done((f32[2,128,512]{2,1,0:T(8,128)}, f32[2,128,512]{2,1,0:T(8,128)S(1)}, u32[]{:S(2)}, u32[]{:S(2)}) %collective-permute-start) | collective-permute-done | bytes 524320 | tf_op jit(solution)/shard_map/ppermute | solution.py:20
  26.0 21.9 %collective-permute-done.2 = f32[2,128,512]{2,1,0:T(8,128)} collective-permute-done((f32[2,128,512]{2,1,0:T(8,128)S(1)}, f32[2,128,512]{2,1,0:T(8,128)}, u32[]{:S(2)}, u32[]{:S(2)}) %collective-permute-start.2) | collective-permute-done | bytes 524320 | tf_op jit(solution)/shard_map/ppermute | solution.py:20
  49.0 2.9 fusion.147
  52.0 2.5 all-gather.26.cloned.1.call-done
  54.5 4.4 fusion.142
  58.9 13.5 %all-gather.34.cloned.1.call-done = f32[1024,512]{1,0:T(8,128)} async-done(((f32[512,512]{1,0:T(8,128)}), f32[1024,512]{1,0:T(8,128)}) %all-gather.34.cloned.1.call-update) | async-done | bytes 2097168 | tf_op jit(solution)/shard_map/all_gather | solution.py:47
  75.6 4.1 fusion.84
  79.9 11.5 %all-gather.28.cloned.1.call-done = f32[1024,512]{1,0:T(8,128)} async-done(((f32[512,512]{1,0:T(8,128)}), f32[1024,512]{1,0:T(8,128)}) %all-gather.28.cloned.1.call-update) | async-done | bytes 2097168 | tf_op jit(solution)/shard_map/all_gather | solution.py:47
  94.6 4.0 fusion.136
  98.7 46.4 %all-gather.36.cloned.1.call-done = f32[2048,512]{1,0:T(8,128)} async-done(((f32[512,512]{1,0:T(8,128)}), f32[2048,512]{1,0:T(8,128)}) %all-gather.36.cloned.1.call-update) | async-done | bytes 4194320 | tf_op jit(solution)/shard_map/all_gather | solution.py:47
  148.5 3.1 fusion.69
  155.4 2.8 fusion.77
  158.7 39.2 %all-gather.30.cloned.1.call-done = f32[2048,512]{1,0:T(8,128)} async-done(((f32[512,512]{1,0:T(8,128)}), f32[2048,512]{1,0:T(8,128)}) %all-gather.30.cloned.1.call-update) | async-done | bytes 4194320 | tf_op jit(solution)/shard_map/all_gather | solution.py:47
  201.3 3.1 fusion.121
  208.3 2.8 fusion.129
  211.5 9.9 %all_gather.88 = f32[2,512]{1,0:T(2,128)S(1)} all-gather(f32[2,128]{1,0:T(2,128)S(1)} %bitcast.347), channel_id=1, replica_groups=mesh['tm_0'=8,'tm_1'=4,'tm_2'=2,'blk'=4] {'blk'}, dimensions={1}, use_global_device_ids=true | all-gather | bytes 5120 | tf_op jit(solution)/shard_map/all_gather | solution.py:74
  222.3 2.4 fusion.82
  224.7 2.4 fusion.15
  233.2 10.4 %all-gather.13 = f32[4,1,512]{2,1,0:T(1,128)S(1)} all-gather(f32[1,1,512]{2,1,0:T(1,128)S(1)} %bitcast.331), channel_id=6, replica_groups=mesh['tm_0'=8,'tm_1'=4,'tm_2'=2,'blk'=4] {'tm_1'}, dimensions={0}, use_global_device_ids=true | all-gather | bytes 10240 | tf_op jit(solution)/shard_map/all_gather | solution.py:47
  247.6 3.0 fusion.20
  254.6 23.5 %all-gather.14 = f32[8,1,512]{2,1,0:T(1,128)S(1)} all-gather(f32[1,1,512]{2,1,0:T(1,128)S(1)} %bitcast.342), channel_id=7, replica_groups=mesh['tm_0'=8,'tm_1'=4,'tm_2'=2,'blk'=4] {'tm_0'}, dimensions={0}, use_global_device_ids=true | all-gather | bytes 18432 | tf_op jit(solution)/shard_map/all_gather | solution.py:47
  279.2 3.0 fusion.6
  282.1 10.2 %all-gather.38.cloned.1.call-done = f32[4096,512]{1,0:T(8,128)} async-done(((f32[512,512]{1,0:T(8,128)}), f32[4096,512]{1,0:T(8,128)}) %all-gather.38.cloned.1.call-update) | async-done | bytes 8388624 | tf_op jit(solution)/shard_map/all_gather | solution.py:47
  294.6 2.5 fusion.29
  297.2 3.1 fusion.39
  300.3 3.1 fusion.43
  316.2 70.8 %all-gather.32.cloned.1.call-done = f32[4096,512]{1,0:T(8,128)} async-done(((f32[512,512]{1,0:T(8,128)}), f32[4096,512]{1,0:T(8,128)}) %all-gather.32.cloned.1.call-update) | async-done | bytes 8388624 | tf_op jit(solution)/shard_map/all_gather | solution.py:47
  391.7 2.5 fusion.97
  400.9 2.4 fusion.113
  426.5 9.7 %all_gather.101 = f32[2,512]{1,0:T(2,128)S(1)} all-gather(f32[2,128]{1,0:T(2,128)S(1)} %bitcast.346), channel_id=1, replica_groups=mesh['tm_0'=8,'tm_1'=4,'tm_2'=2,'blk'=4] {'blk'}, dimensions={1}, use_global_device_ids=true | all-gather | bytes 5120 | tf_op jit(solution)/shard_map/all_gather | solution.py:94
  440.0 11.4 %all-gather.16 = f32[4,1,512]{2,1,0:T(1,128)S(1)} all-gather(f32[1,1,512]{2,1,0:T(1,128)S(1)} %bitcast.330), channel_id=12, replica_groups=mesh['tm_0'=8,'tm_1'=4,'tm_2'=2,'blk'=4] {'tm_1'}, dimensions={0}, use_global_device_ids=true | all-gather | bytes 10240 | tf_op jit(solution)/shard_map/all_gather | solution.py:47
  455.5 23.3 %all-gather.17 = f32[8,1,512]{2,1,0:T(1,128)S(1)} all-gather(f32[1,1,512]{2,1,0:T(1,128)S(1)} %bitcast.337), channel_id=13, replica_groups=mesh['tm_0'=8,'tm_1'=4,'tm_2'=2,'blk'=4] {'tm_0'}, dimensions={0}, use_global_device_ids=true | all-gather | bytes 18432 | tf_op jit(solution)/shard_map/all_gather | solution.py:47
  (214 shorter events, 122.6 us)
Async XLA Ops:
  7.2 418.8 %copy-start = (f32[2,128,512]{2,1,0:T(8,128)S(1)}, f32[2,128,512]{2,1,0:T(8,128)}, u32[]{:S(2)}) copy-start(f32[2,128,512]{2,1,0:T(8,128)} %param.11) | copy-start | bytes 1572868
  7.2 47.3 %all-gather.26.cloned.1.call-start = ((), (), s32[]{:S(2)}) async-start(), calls=%async_computation | async-start | bytes 2621440 | tf_op jit(solution)/shard_map/all_gather | solution.py:72
  7.9 64.5 %all-gather.34.cloned.1.call-start = ((), (), s32[]{:S(2)}) async-start(), calls=%async_computation.4 | async-start | bytes 3145728 | tf_op jit(solution)/shard_map/all_gather | solution.py:47
  8.0 15.2 %collective-permute-start = (f32[2,128,512]{2,1,0:T(8,128)}, f32[2,128,512]{2,1,0:T(8,128)S(1)}, u32[]{:S(2)}, u32[]{:S(2)}) collective-permute-start(f32[2,128,512]{2,1,0:T(8,128)} %param.10), channel_id=1, source_target_pairs={{0,1},{1,2},{2,3},{3,0},{4,5},{5,6},{6,7},{7,4},{8,9},{9,10},{10,1... | collective-permute-start | bytes 1572872 | tf_op jit(solution)/shard_map/ppermute | solution.py:20
  9.6 15.3 %collective-permute-start.1 = (f32[2,128,512]{2,1,0:T(8,128)}, f32[2,128,512]{2,1,0:T(8,128)}, u32[]{:S(2)}, u32[]{:S(2)}) collective-permute-start(f32[2,128,512]{2,1,0:T(8,128)} %param.10), channel_id=1, source_target_pairs={{0,3},{1,0},{2,1},{3,2},{4,7},{5,4},{6,5},{7,6},{8,11},{9,8},{10,9... | collective-permute-start | bytes 1572872 | tf_op jit(solution)/shard_map/ppermute | solution.py:27
  23.2 24.8 %collective-permute-start.2 = (f32[2,128,512]{2,1,0:T(8,128)S(1)}, f32[2,128,512]{2,1,0:T(8,128)}, u32[]{:S(2)}, u32[]{:S(2)}) collective-permute-start(f32[2,128,512]{2,1,0:T(8,128)S(1)} %collective-permute-done), channel_id=1, source_target_pairs={{0,1},{1,2},{2,3},{3,0},{4,5},{5,6},{6,7},{7,4},{8,9},{9,10},{10,1... | collective-permute-start | bytes 1572872 | tf_op jit(solution)/shard_map/ppermute | solution.py:20
  51.9 39.5 %all-gather.28.cloned.1.call-start = ((), (), s32[]{:S(2)}) async-start(), calls=%async_computation.1 | async-start | bytes 3145728 | tf_op jit(solution)/shard_map/all_gather | solution.py:47
  58.9 86.3 %all-gather.36.cloned.1.call-start = ((), (), s32[]{:S(2)}) async-start(), calls=%async_computation.5 | async-start | bytes 5242880 | tf_op jit(solution)/shard_map/all_gather | solution.py:47
  79.7 118.3 %all-gather.30.cloned.1.call-start = ((), (), s32[]{:S(2)}) async-start(), calls=%async_computation.2 | async-start | bytes 5242880 | tf_op jit(solution)/shard_map/all_gather | solution.py:47
  98.7 193.6 %all-gather.38.cloned.1.call-start = ((), (), s32[]{:S(2)}) async-start(), calls=%async_computation.6 | async-start | bytes 9437184 | tf_op jit(solution)/shard_map/all_gather | solution.py:47
  158.3 228.7 %all-gather.32.cloned.1.call-start = ((), (), s32[]{:S(2)}) async-start(), calls=%async_computation.3 | async-start | bytes 9437184 | tf_op jit(solution)/shard_map/all_gather | solution.py:47
  197.9 7.4 %copy-start.7 = (f32[2048,512]{1,0:T(8,128)S(1)}, f32[2048,512]{1,0:T(8,128)}, u32[]{:S(2)}) copy-start(f32[2048,512]{1,0:T(8,128)} %all-gather.30.cloned.1.call-done) | copy-start | bytes 12582916
  211.1 16.0 %copy-start.3 = (f32[2,512,512]{2,1,0:T(8,128)S(1)}, f32[2,512,512]{2,1,0:T(8,128)}, u32[]{:S(2)}) copy-start(f32[2,512,512]{2,1,0:T(8,128)} %all-gather.26.cloned.1.call-done) | copy-start | bytes 6291460
  211.2 20.0 %copy-start.33 = (f32[1024,512]{1,0:T(8,128)S(1)}, f32[1024,512]{1,0:T(8,128)}, u32[]{:S(2)}) copy-start(f32[1024,512]{1,0:T(8,128)} %all-gather.28.cloned.1.call-done) | copy-start | bytes 6291460
  222.3 21.6 %copy-start.14 = (f32[512,512]{1,0:T(8,128)S(1)}, f32[512,512]{1,0:T(8,128)}, u32[]{:S(2)}) copy-start(f32[512,512]{1,0:T(8,128)} %copy-done.13) | copy-start | bytes 3145732
  222.3 21.6 %copy-start.15 = (f32[512,512]{1,0:T(8,128)S(1)}, f32[512,512]{1,0:T(8,128)}, u32[]{:S(2)}) copy-start(f32[512,512]{1,0:T(8,128)} %fusion.136) | copy-start | bytes 3145732
  227.1 20.4 %copy-start.30 = (f32[512,512]{1,0:T(8,128)}, f32[512,512]{1,0:T(8,128)S(1)}, u32[]{:S(2)}) copy-start(f32[512,512]{1,0:T(8,128)S(1)} %fusion.15) | copy-start | bytes 3145732
  227.2 20.4 %copy-start.17 = (f32[512,512]{1,0:T(8,128)S(1)}, f32[512,512]{1,0:T(8,128)}, u32[]{:S(2)}) copy-start(f32[512,512]{1,0:T(8,128)} %copy-done.16) | copy-start | bytes 3145732
  227.2 20.4 %copy-start.19 = (f32[512,512]{1,0:T(8,128)S(1)}, f32[512,512]{1,0:T(8,128)}, u32[]{:S(2)}) copy-start(f32[512,512]{1,0:T(8,128)} %copy-done.18) | copy-start | bytes 3145732
  227.2 20.4 %copy-start.24 = (f32[512,512]{1,0:T(8,128)S(1)}, f32[512,512]{1,0:T(8,128)}, u32[]{:S(2)}) copy-start(f32[512,512]{1,0:T(8,128)} %fusion.77) | copy-start | bytes 3145732
  227.2 20.4 %copy-start.28 = (f32[512,512]{1,0:T(8,128)S(1)}, f32[512,512]{1,0:T(8,128)}, u32[]{:S(2)}) copy-start(f32[512,512]{1,0:T(8,128)} %copy-done.27) | copy-start | bytes 3145732
  250.6 28.5 %copy-start.10 = (f32[512,512]{1,0:T(8,128)S(1)}, f32[512,512]{1,0:T(8,128)}, u32[]{:S(2)}) copy-start(f32[512,512]{1,0:T(8,128)} %copy-done.9) | copy-start | bytes 3145732
  250.6 28.6 %copy-start.12 = (f32[512,512]{1,0:T(8,128)S(1)}, f32[512,512]{1,0:T(8,128)}, u32[]{:S(2)}) copy-start(f32[512,512]{1,0:T(8,128)} %copy-done.11) | copy-start | bytes 3145732
  250.6 28.6 %copy-start.23 = (f32[512,512]{1,0:T(8,128)S(1)}, f32[512,512]{1,0:T(8,128)}, u32[]{:S(2)}) copy-start(f32[512,512]{1,0:T(8,128)} %fusion.129) | copy-start | bytes 3145732
  250.6 28.6 %copy-start.26 = (f32[512,512]{1,0:T(8,128)S(1)}, f32[512,512]{1,0:T(8,128)}, u32[]{:S(2)}) copy-start(f32[512,512]{1,0:T(8,128)} %copy-done.25) | copy-start | bytes 3145732
  292.3 11.1 %copy-start.1 = (f32[4096,512]{1,0:T(8,128)S(1)}, f32[4096,512]{1,0:T(8,128)}, u32[]{:S(2)}) copy-start(f32[4096,512]{1,0:T(8,128)} %all-gather.38.cloned.1.call-done) | copy-start | bytes 25165828
  387.0 18.5 %copy-start.29 = (f32[512,512]{1,0:T(8,128)S(1)}, f32[512,512]{1,0:T(8,128)}, u32[]{:S(2)}) copy-start(f32[512,512]{1,0:T(8,128)} %fusion.6) | copy-start | bytes 3145732
  389.3 17.2 %copy-start.2 = (f32[4096,512]{1,0:T(8,128)S(1)}, f32[4096,512]{1,0:T(8,128)}, u32[]{:S(2)}) copy-start(f32[4096,512]{1,0:T(8,128)} %all-gather.32.cloned.1.call-done) | copy-start | bytes 25165828
  418.9 20.1 %copy-start.32 = (f32[1024,512]{1,0:T(8,128)S(1)}, f32[1024,512]{1,0:T(8,128)}, u32[]{:S(2)}) copy-start(f32[1024,512]{1,0:T(8,128)} %all-gather.34.cloned.1.call-done) | copy-start | bytes 6291460
  421.1 30.4 %copy-start.6 = (f32[2048,512]{1,0:T(8,128)S(1)}, f32[2048,512]{1,0:T(8,128)}, u32[]{:S(2)}) copy-start(f32[2048,512]{1,0:T(8,128)} %all-gather.36.cloned.1.call-done) | copy-start | bytes 12582916
  423.9 30.5 %copy-start.31 = (f32[512,512]{1,0:T(8,128)S(1)}, f32[512,512]{1,0:T(8,128)}, u32[]{:S(2)}) copy-start(f32[512,512]{1,0:T(8,128)} %copy-done.30) | copy-start | bytes 3145732
  454.5 39.9 %copy-start.22 = (f32[512,512]{1,0:T(8,128)S(1)}, f32[512,512]{1,0:T(8,128)}, u32[]{:S(2)}) copy-start(f32[512,512]{1,0:T(8,128)} %fusion.20) | copy-start | bytes 3145732
  (16 other events, 45.5 us)
Sparse Core Ops, SparseCore 0:
  9.8 44.6 all-gather.25
  56.3 16.0 all-gather.33
  74.2 17.1 all-gather.27
  93.1 52.0 all-gather.35
  146.8 51.0 all-gather.29
  199.6 92.6 all-gather.37
  294.1 92.9 all-gather.31
